TPU v7x, 128 devices: a whole 4x4x4 slice. The times are simulated.
128 devices in a mesh: obs: 8 (over y, core), src: 16 (over x, z).
Axes of the slice: x: 4, y: 4, z: 4, core: 2. Of those that a mesh axis runs over, the one named last changes fastest.
Arguments:
- data: float32 [1024, 1536], P(('obs', 'src')), may hold values from -170 to 170
- obs_points: float32 [1024, 3, 256], P('obs'), may hold values from 0 to 32, as said below
- src_points: float32 [1024, 3, 256], P('src'), may hold values from -0.4 to 32, as said below
- obs_basis: float32 [1024, 64, 1536], P(('obs', 'src')), may hold values from -0.09375 to 0.09375
- src_basis: float32 [1024, 64, 256], P(('src', 'obs')), may hold values from -0.375 to 0.375
- couplings: float32 [8, 16, 320, 64, 64], P('obs', 'src'), may hold values from -0.75 to 0.75
- near_pairs: int32 [8, 16, 72], P('obs', 'src'), may hold values from -1 to 8191, as said below
- far_pairs: int32 [8, 16, 320], P('obs', 'src'), may hold values from -1 to 8191, as said below
Outputs:
- sources: float32 [1024, 256], P(('src', 'obs'))
- residual: float32 [1024, 1536], P(('obs', 'src'))
- normal_residual: float32 [1024, 256], P(('src', 'obs'))
- misfit: float32 [3], replicated
Inputs may be any that keep to these rules, and one draw needn't show every extreme that they name: Live entries of every block come first and -1 fills the remaining slots; a live entry o * 64 + s pairs local observation leaf o with local source leaf s; no pair is listed twice, and no pair is in both near_pairs and far_pairs. Leaves lie on surface tiles: observation leaf n on tile row (n // 32 + c) % 32, tile column n % 32, with one c of 0 to 3 for all leaves of a draw; source leaf m = j * 64 + h * 8 + l (0 <= h < 8, 0 <= l < 8) on tile row (l % 4) * 8 + h, tile column j * 2 + l // 4. A near pair joins two leaves whose tile rows differ by at most one and whose tile columns differ by at most one. `far_pairs`: live entries of every block come first and -1 fills the remaining slots; a live entry o * 64 + s pairs local observation leaf o with local source leaf s, coupled by the matrix in the same slot of couplings; no pair is listed twice; on the tiles described for near_pairs, the larger of its two leaves' tile row and tile column differences is two or three. `obs_points`: the third coordinate of every observation point lies in [0.5, 0.9]. `src_points`: the third coordinate of every source lies in [-0.4, -0.1].
All inputs are finite; a program needn't handle non-finite values.
Results may differ from a plain program's by a relative error of at most 0.0003.
Values sent between devices are 32-bit elements; how exact they have to be, the bound alone decides.
No kernel may reach another device: no remote copies, remote signals or barrier semaphores. Data moves between devices by JAX's collectives and lax.ppermute only.
A program may use at most 128 MiB of HBM per device.

v0:
```python
import jax
import jax.numpy as jnp
from jax import lax
from jax.sharding import Mesh
from jax.sharding import PartitionSpec as P

ITERS = 2
OBS_SRC = ("obs_0", "obs_1", "src_0", "src_1")
SRC = ("src_0", "src_1")
OBS = ("obs_0", "obs_1")
SRC_OBS = ("src_0", "src_1", "obs_0", "obs_1")
exact = lax.Precision.HIGHEST


def over_axes(value, axes):
    for axis in axes:
        value = lax.psum(value, axis)
    return value


def from_everyone(value, axis):
    copies = jnp.broadcast_to(value, (lax.axis_size(axis), *value.shape))
    return lax.all_to_all(copies, axis, split_axis=0, concat_axis=0, tiled=True)


def laid_out(pieces, dim):
    lengths = list(pieces.shape[1:])
    lengths[dim] *= pieces.shape[0]
    return jnp.moveaxis(pieces, 0, dim).reshape(lengths)


def gathered_copies(value, axis, dim):
    pieces = from_everyone(value, axis)
    return laid_out(pieces, dim)


def side_by_side(arrays, axis, dim, along):
    ends, at = ([], 0)
    for a in arrays[:-1]:
        at += a.shape[along]
        ends.append(at)
    both = jnp.concatenate(arrays, axis=along)
    return tuple(jnp.split(lax.all_gather(both, axis, axis=dim, tiled=True), ends, axis=along))


def cut_along(value, dim, devices):
    before, after = (value.shape[:dim], value.shape[dim + 1 :])
    return jnp.moveaxis(value.reshape(*before, devices, -1, *after), dim, 0)


def summed_on_arrival(value, axis, dim):
    pieces = cut_along(value, dim, lax.axis_size(axis))
    arrived = lax.all_to_all(pieces, axis, split_axis=0, concat_axis=0, tiled=True)
    return arrived.sum(axis=0)


def sent_together(arrays, axis, dim, along):
    widths = [a.shape[along] for a in arrays]
    both = jnp.concatenate(arrays, axis=along)
    out = summed_on_arrival(both, axis, dim)
    return tuple(jnp.split(out, [sum(widths[:k]) for k in range(1, len(widths))], axis=along))


def tensor_parts(obs_pts, src_pts):
    diff_x = obs_pts[:, 0, :, None] - src_pts[:, 0, None, :]
    diff_y = obs_pts[:, 1, :, None] - src_pts[:, 1, None, :]
    diff_z = obs_pts[:, 2, :, None] - src_pts[:, 2, None, :]
    inverse = lax.rsqrt(diff_x * diff_x + diff_y * diff_y + diff_z * diff_z)
    inv_cube = inverse * inverse * inverse / obs_pts.shape[-1]
    inv_fifth = 3.0 * inv_cube * inverse * inverse
    return (
        inv_fifth * diff_x * diff_x - inv_cube,
        inv_fifth * diff_x * diff_y,
        inv_fifth * diff_x * diff_z,
        inv_fifth * diff_y * diff_y - inv_cube,
        inv_fifth * diff_y * diff_z,
        inv_fifth * diff_z * diff_z - inv_cube,
    )


def near_loop(obs_ids, src_ids, pair_count, obs_pts, src_pts, source, target, forward, group_size):
    length = obs_ids.shape[0]
    padding = -length % group_size
    obs_ids = jnp.concatenate([obs_ids, jnp.zeros((padding,), jnp.int32)])
    src_ids = jnp.concatenate([src_ids, jnp.zeros((padding,), jnp.int32)])

    def one_group(group_index, running):
        first_slot = (group_index * group_size).astype(jnp.int32)
        obs_take = lax.dynamic_slice_in_dim(obs_ids, first_slot, group_size)
        src_take = lax.dynamic_slice_in_dim(src_ids, first_slot, group_size)
        in_range = first_slot + jnp.arange(group_size, dtype=jnp.int32) < pair_count
        tensor = tensor_parts(obs_pts[obs_take], src_pts[src_take])
        if forward:
            strengths = jnp.where(in_range[:, None], source[src_take], 0.0)[:, None, :]
            contributions = jnp.stack(
                [jnp.sum(component * strengths, axis=2) for component in tensor], axis=1
            )
            return running.at[obs_take].add(contributions.reshape(group_size, -1))
        residual_rows = jnp.where(in_range[:, None], source[obs_take], 0.0).reshape(
            group_size, 6, -1
        )
        weighted = tensor[0] * residual_rows[:, 0, :, None]
        for which in range(1, 6):
            weighted = weighted + tensor[which] * residual_rows[:, which, :, None]
        return running.at[src_take].add(jnp.sum(weighted, axis=1))

    groups = (pair_count + group_size - 1) // group_size
    return lax.fori_loop(0, groups, one_group, target)


def compact(chosen):
    length = chosen.shape[0]
    position = jnp.cumsum(chosen.astype(jnp.int32)) - 1
    target = jnp.where(chosen, position, length)
    picked = (
        jnp.zeros((length,), jnp.int32)
        .at[target]
        .set(jnp.arange(length, dtype=jnp.int32), mode="drop")
    )
    return (picked, jnp.sum(chosen.astype(jnp.int32)))


def global_total(value):
    return over_axes(value, OBS_SRC)


def paired_totals(first, second):
    return (over_axes(first, OBS_SRC), over_axes(second, OBS_SRC))


def shards(data, obs_points, src_points, obs_basis, src_basis, couplings, near_pairs, far_pairs):
    own_rows = data.shape[0]
    obs_sub = obs_points.shape[0]
    src_sub = src_points.shape[0]
    leaf_size = obs_points.shape[-1]
    rank_size = src_basis.shape[1]
    capacity = near_pairs.shape[-1]
    group_size = 8
    column = lax.axis_index(SRC)
    coupling = couplings[0, 0]
    far_list = far_pairs[0, 0]
    far_live = far_list >= 0
    far_safe = jnp.where(far_live, far_list, 0)
    far_obs = far_safe // src_sub
    far_src = far_safe % src_sub
    row_lists = gathered_copies(near_pairs, SRC, 1)[0].reshape(-1)
    all_points = lax.all_gather(src_points, SRC, axis=0, tiled=True)
    slot_ids = jnp.arange(row_lists.shape[0], dtype=jnp.int32)
    row_safe = jnp.where(row_lists >= 0, row_lists, 0)
    local_obs = row_safe // src_sub
    owned = (row_lists >= 0) & (local_obs // own_rows == column)
    picked, near_count = compact(owned)
    near_obs = jnp.clip(local_obs[picked] - column * own_rows, 0, own_rows - 1)
    near_src = slot_ids[picked] // capacity * src_sub + row_safe[picked] % src_sub
    own_points = lax.dynamic_slice_in_dim(obs_points, column * own_rows, own_rows)

    def far_adjoint(coeff_sub):
        chosen_coeffs = jnp.where(far_live[:, None], coeff_sub[far_obs], 0.0)
        far_terms = jnp.einsum("ckl,ck->cl", coupling, chosen_coeffs, precision=exact)
        return jnp.zeros((src_sub, rank_size), jnp.float32).at[far_src].add(far_terms)

    def apply_adjoint(values):
        coeff_own = jnp.einsum("nkm,nm->nk", obs_basis, values, precision=exact)
        coeff_sub = gathered_copies(coeff_own, SRC, 0)
        near_all = near_loop(
            near_obs,
            near_src,
            near_count,
            own_points,
            all_points,
            values,
            jnp.zeros((all_points.shape[0], leaf_size), jnp.float32),
            False,
            group_size,
        )
        near_block = summed_on_arrival(near_all, SRC, 0)
        coeff_src = far_adjoint(coeff_sub)
        near_own, coeff_back = sent_together((near_block, coeff_src), OBS, 0, 1)
        return near_own + jnp.einsum("nk,nkq->nq", coeff_back, src_basis, precision=exact)

    residual = data
    normal = apply_adjoint(residual)
    gamma_now = global_total(jnp.sum(normal * normal))
    misfit_now = global_total(jnp.sum(residual * residual))
    history = [misfit_now]
    direction = normal
    solution = jnp.zeros_like(normal)
    for iteration in range(ITERS):
        apply_coeff_own = jnp.einsum("nkq,nq->nk", src_basis, direction, precision=exact)
        gathered, apply_coeff_sub = side_by_side((direction, apply_coeff_own), OBS, 0, 1)
        far_chosen_coeffs = jnp.where(far_live[:, None], apply_coeff_sub[far_src], 0.0)
        far_far_terms = jnp.einsum("ckl,cl->ck", coupling, far_chosen_coeffs, precision=exact)
        coeff_obs = jnp.zeros((obs_sub, rank_size), jnp.float32).at[far_obs].add(far_far_terms)
        everything = gathered_copies(gathered, SRC, 0)
        apply_coeff_back = summed_on_arrival(coeff_obs, SRC, 0)
        apply_near_own = near_loop(
            near_obs,
            near_src,
            near_count,
            own_points,
            all_points,
            everything,
            jnp.zeros((own_rows, 6 * leaf_size), jnp.float32),
            True,
            group_size,
        )
        projected = apply_near_own + jnp.einsum(
            "nk,nkm->nm", apply_coeff_back, obs_basis, precision=exact
        )
        curvature, cross_term = paired_totals(
            jnp.sum(projected * projected), jnp.sum(residual * projected)
        )
        step_size = gamma_now / curvature
        solution = solution + step_size * direction
        residual = residual - step_size * projected
        misfit_now = misfit_now - 2.0 * step_size * cross_term + step_size * step_size * curvature
        history.append(misfit_now)
        normal = apply_adjoint(residual)
        gamma_next = global_total(jnp.sum(normal * normal))
        direction = normal + gamma_next / gamma_now * direction
        gamma_now = gamma_next
    return (solution, residual, normal, jnp.stack(history))


def solution(mesh):
    finer = Mesh(mesh.devices.reshape(4, 2, 4, 4), ("obs_0", "obs_1", "src_0", "src_1"))
    return jax.shard_map(
        shards,
        mesh=finer,
        in_specs=(
            P(OBS_SRC, None),
            P(OBS, None, None),
            P(SRC, None, None),
            P(OBS_SRC, None, None),
            P(SRC_OBS, None, None),
            P(OBS, SRC, None, None, None),
            P(OBS, SRC, None),
            P(OBS, SRC, None),
        ),
        out_specs=(P(SRC_OBS, None), P(OBS_SRC, None), P(SRC_OBS, None), P()),
        check_vma=False,
    )
```

profile of v0, /device:TPU:1, one launch (start us, length us, event | category | flops | bytes accessed | tf_op | source)
XLA Modules:
  0.0 791.0 jit_solution(15774144450242854606)
XLA Ops:
  9.4 8.4 %all-to-all-start = ((s32[16,1,1,72]{3,2,1,0:T(1,128)}), s32[16,1,1,72]{3,2,1,0:T(1,128)S(1)}, u32[]{:S(2)}, u32[]{:S(2)}) async-start(s32[16,1,1,72]{3,2,1,0:T(1,128)} %broadcast_in_dim.201), calls=%async_computation | async-start | bytes 16384 | tf_op jit(solution)/shard_map/all_to_all | solution.py:23
  24.2 5.4 all-to-all-start.2
  33.1 6.4 scatter_custom_fusion.5
  39.6 6.5 gather_fusion.16
  46.1 6.5 gather_fusion.17
  52.6 6.5 gather_fusion.15
  60.9 6.0 copy.23
  67.9 45.0 %while.60 = (s32[]{:T(128)}, f32[1024,256]{1,0:T(8,128)}, s32[]{:T(128)}, s32[1152]{0:T(1024)S(1)}, s32[1152]{0:T(1024)S(1)}, /*index=5*/f32[8,3,256]{2,1,0:T(4,...) while((s32[]{:T(128)}, f32[1024,256]{1,0:T(8,128)}, ...), condition=%wide.region_7.8_spmd, body=%wide.region_4.7_spmd.sunk | while | flops 19937348 | bytes 729607 | solution.py:108
  72.8 3.6 fusion.193
  84.1 3.6 fusion.193
  95.3 3.6 fusion.193
  106.6 3.6 fusion.193
  113.0 27.6 %all-to-all-start.1 = ((f32[16,64,256]{2,1,0:T(8,128)}), f32[16,64,256]{2,1,0:T(8,128)}, u32[]{:S(2)}, u32[]{:S(2)}) async-start(f32[16,64,256]{2,1,0:T(8,128)} %bitcast.406), calls=%async_computation.1 | async-start | bytes 2097152 | tf_op jit(solution)/shard_map/all_to_all | solution.py:53
  140.7 12.4 %copy.31 = f32[320,64,64]{2,1,0:T(8,128)} copy(f32[320,64,64]{0,2,1:T(8,128)} %bitcast.404) | data formatting | bytes 10485760 | tf_op jit(solution)/shard_map/squeeze | solution.py:140
  153.1 12.5 %copy.38 = f32[320,64,64]{1,2,0:T(8,128)} copy(f32[320,64,64]{0,2,1:T(8,128)} %bitcast.405) | data formatting | bytes 10485760 | tf_op jit(solution)/shard_map/squeeze | solution.py:140
  168.2 11.5 %fusion.141 = f32[320,1,64]{2,1,0:T(1,128)S(1)} fusion(f32[320,64,1]{1,2,0:T(1,128)S(1)} %bitcast.416, f32[320,64,64]{2,1,0:T(8,128)} %copy.31), kind=kOutput, calls=%fused_computation.424 | convolution fusion | flops 15728640 | bytes 5406720 | tf_op jit(solution)/shard_map/ckl,ck->cl/dot_general | solution.py:159
  184.1 4.3 all-to-all-start.3
  188.4 5.0 all-to-all-done.3
  197.0 13.8 %all_gather.10 = f32[64,320]{1,0:T(8,128)S(1)} all-gather(f32[8,320]{1,0:T(8,128)S(1)} %pad_maximum_fusion), channel_id=1, replica_groups=mesh['obs_0'=4,'obs_1'=2,'src_0'=4,'src_1'=4] {'obs_0','obs_1'}, dimensions={0}, use_global_device_ids=true | all-gather | bytes 92160 | tf_op jit(solution)/shard_map/all_gather | solution.py:43
  212.0 12.2 %fusion.143 = f32[320,1,64]{2,1,0:T(1,128)} fusion(f32[320,64,1]{1,2,0:T(1,128)S(1)} %bitcast.417, f32[320,64,64]{1,2,0:T(8,128)} %copy.38), kind=kOutput, calls=%fused_computation.426 | convolution fusion | flops 15728640 | bytes 5406720 | tf_op jit(solution)/shard_map/ckl,cl->ck/dot_general | solution.py:192
  227.7 6.4 all-to-all-start.5
  234.2 6.5 all-to-all-done.5
  241.7 4.4 all-to-all-start.4
  248.5 12.9 %all-to-all-done.4 = f32[16,64,256]{2,1,0:T(8,128)} async-done(((f32[16,64,256]{2,1,0:T(8,128)}), f32[16,64,256]{2,1,0:T(8,128)}, u32[]{:S(2)}, u32[]{:S(2)}) %all-to-all-start.4) | async-done | bytes 1048608 | tf_op jit(solution)/shard_map/all_to_all | solution.py:23
  261.4 44.4 %while.61 = (s32[]{:T(128)}, f32[8,1536]{1,0:T(8,128)S(1)}, s32[]{:T(128)}, s32[1152]{0:T(1024)S(1)}, f32[8,3,256]{2,1,0:T(4,128)S(1)}, /*index=5*/s32[1152]{0:T...) while((s32[]{:T(128)}, f32[8,1536]{1,0:T(8,128)S(1)}, ...), condition=%wide.region_24.25_spmd, body=%wide.region_16.24_spmd.sunk | while | flops 19927108 | bytes 688647 | solution.py:108
  267.6 4.2 fusion.196
  278.7 4.2 fusion.196
  289.8 4.2 fusion.196
  300.9 4.2 fusion.196
  306.5 18.9 %all-reduce.5 = (f32[]{:T(128)}, f32[]{:T(128)}) all-reduce(f32[]{:T(128)} %get-tuple-element.814, f32[]{:T(128)} %get-tuple-element.694), channel_id=1, replica_groups=mesh['obs_0'=4,'obs_1'=2,'src_0'=4,'src_1'=4] {'obs_0'}, use_global_device_ids=true, to_apply=%region_12.13 | all-reduce | flops 2 | bytes 16 | tf_op jit(solution)/shard_map/psum | solution.py:17
  325.4 17.3 %all-reduce.7 = (f32[]{:T(128)}, f32[]{:T(128)}) all-reduce(f32[]{:T(128)} %get-tuple-element.806, f32[]{:T(128)} %get-tuple-element.807), channel_id=1, replica_groups=mesh['obs_0'=4,'obs_1'=2,'src_0'=4,'src_1'=4] {'obs_1'}, use_global_device_ids=true, to_apply=%region_13.14 | all-reduce | flops 2 | bytes 16 | tf_op jit(solution)/shard_map/psum | solution.py:17
  342.8 6.7 all-reduce.3
  349.5 6.9 all-reduce.1
  361.1 4.2 all-to-all-start.7
  366.5 45.4 %while.62 = (s32[]{:T(128)}, f32[1024,256]{1,0:T(8,128)}, s32[]{:T(128)}, s32[1152]{0:T(1024)S(1)}, s32[1152]{0:T(1024)S(1)}, /*index=5*/f32[8,3,256]{2,1,0:T(4,...) while((s32[]{:T(128)}, f32[1024,256]{1,0:T(8,128)}, ...), condition=%wide.region_35.36_spmd, body=%wide.region_32.35_spmd.sunk | while | flops 19937348 | bytes 729607 | solution.py:108
  405.4 3.6 fusion.199
  411.9 29.2 %all-to-all-start.6 = ((f32[16,64,256]{2,1,0:T(8,128)}), f32[16,64,256]{2,1,0:T(8,128)}, u32[]{:S(2)}, u32[]{:S(2)}) async-start(f32[16,64,256]{2,1,0:T(8,128)} %bitcast.407), calls=%async_computation.6 | async-start | bytes 2097152 | tf_op jit(solution)/shard_map/all_to_all | solution.py:53
  443.1 11.5 %fusion.145 = f32[320,1,64]{2,1,0:T(1,128)S(1)} fusion(f32[320,64,1]{1,2,0:T(1,128)S(1)} %bitcast.418, f32[320,64,64]{2,1,0:T(8,128)} %copy.31), kind=kOutput, calls=%fused_computation.428 | convolution fusion | flops 15728640 | bytes 5406720 | tf_op jit(solution)/shard_map/ckl,ck->cl/dot_general | solution.py:159
  458.5 9.7 %all_to_all.70 = f32[8,8,320]{2,1,0:T(8,128)S(1)} all-to-all(f32[8,8,320]{2,1,0:T(8,128)S(1)} %maximum_bitcast_fusion.1), channel_id=1, replica_groups=mesh['obs_0'=4,'obs_1'=2,'src_0'=4,'src_1'=4] {'obs_0','obs_1'}, dimensions={0} | all-to-all | bytes 163840 | tf_op jit(solution)/shard_map/all_to_all | solution.py:53
  470.3 7.5 psum.204
  477.7 5.6 psum.205
  483.3 9.1 %psum.206 = f32[]{:T(128)} all-reduce(f32[]{:T(128)} %psum.205), channel_id=1, replica_groups=mesh['obs_0'=4,'obs_1'=2,'src_0'=4,'src_1'=4] {'src_0'}, use_global_device_ids=true, to_apply=%region_42.43 | all-reduce | flops 1 | bytes 8 | tf_op jit(solution)/shard_map/psum | solution.py:17
  492.4 9.3 %psum.207 = f32[]{:T(128)} all-reduce(f32[]{:T(128)} %psum.206), channel_id=1, replica_groups=mesh['obs_0'=4,'obs_1'=2,'src_0'=4,'src_1'=4] {'src_1'}, use_global_device_ids=true, to_apply=%region_43.44 | all-reduce | flops 1 | bytes 8 | tf_op jit(solution)/shard_map/psum | solution.py:17
  504.6 17.2 %all_gather.11 = f32[64,320]{1,0:T(8,128)S(1)} all-gather(f32[8,320]{1,0:T(8,128)S(1)} %pad_maximum_fusion.1), channel_id=1, replica_groups=mesh['obs_0'=4,'obs_1'=2,'src_0'=4,'src_1'=4] {'obs_0','obs_1'}, dimensions={0}, use_global_device_ids=true | all-gather | bytes 92160 | tf_op jit(solution)/shard_map/all_gather | solution.py:43
  523.8 12.2 %fusion.147 = f32[320,1,64]{2,1,0:T(1,128)} fusion(f32[320,64,1]{1,2,0:T(1,128)S(1)} %bitcast.415, f32[320,64,64]{1,2,0:T(8,128)} %copy.38), kind=kOutput, calls=%fused_computation.430 | convolution fusion | flops 15728640 | bytes 5406720 | tf_op jit(solution)/shard_map/ckl,cl->ck/dot_general | solution.py:192
  543.0 6.4 all-to-all-done.10
  550.4 4.3 all-to-all-start.9
  557.2 13.0 %all-to-all-done.9 = f32[16,64,256]{2,1,0:T(8,128)} async-done(((f32[16,64,256]{2,1,0:T(8,128)}), f32[16,64,256]{2,1,0:T(8,128)}, u32[]{:S(2)}, u32[]{:S(2)}) %all-to-all-start.9) | async-done | bytes 1048608 | tf_op jit(solution)/shard_map/all_to_all | solution.py:23
  570.3 44.4 %while.63 = (s32[]{:T(128)}, f32[8,1536]{1,0:T(8,128)S(1)}, s32[]{:T(128)}, s32[1152]{0:T(1024)S(1)}, f32[8,3,256]{2,1,0:T(4,128)S(1)}, /*index=5*/s32[1152]{0:T...) while((s32[]{:T(128)}, f32[8,1536]{1,0:T(8,128)S(1)}, ...), condition=%wide.region_52.53_spmd, body=%wide.region_44.52_spmd.sunk | while | flops 19927108 | bytes 688647 | solution.py:108
  576.4 4.2 fusion.202
  587.5 4.2 fusion.202
  598.6 4.2 fusion.202
  609.7 4.2 fusion.202
  615.3 18.6 %all-reduce.4 = (f32[]{:T(128)}, f32[]{:T(128)}, f32[]{:T(128)}, f32[]{:T(128)}) all-reduce(f32[]{:T(128)} %get-tuple-element.692, f32[]{:T(128)} %get-tuple-element.695, f32[]{:T(128)} %get-tuple-element.693, f32[]{:T(128)} %get-tuple-element.691), channel_id=1, replica_groups=mesh['obs_0'=4,'obs_1'=2,'src_0'=4,'src_1'=4] {'obs_0'}, use_global_device_ids=true, to_apply=%region_56.57 | all-reduce | flops 4 | bytes 32 | tf_op jit(solution)/shard_map/psum | solution.py:17
  633.9 17.8 %all-reduce.6 = (f32[]{:T(128)}, f32[]{:T(128)}, f32[]{:T(128)}, f32[]{:T(128)}) all-reduce(f32[]{:T(128)} %get-tuple-element.802, f32[]{:T(128)} %get-tuple-element.803, f32[]{:T(128)} %get-tuple-element.804, f32[]{:T(128)} %get-tuple-element.805), channel_id=1, replica_groups=mesh['obs_0'=4,'obs_1'=2,'src_0'=4,'src_1'=4] {'obs_1'}, use_global_device_ids=true, to_apply=%region_57.58 | all-reduce | flops 4 | bytes 32 | tf_op jit(solution)/shard_map/psum | solution.py:17
  651.7 6.7 all-reduce.2
  658.4 6.9 all-reduce
  670.1 4.2 all-to-all-start.12
  675.3 45.0 %while.64 = (s32[]{:T(128)}, f32[1024,256]{1,0:T(8,128)}, s32[]{:T(128)}, s32[1152]{0:T(1024)S(1)}, s32[1152]{0:T(1024)S(1)}, /*index=5*/f32[8,3,256]{2,1,0:T(4,...) while((s32[]{:T(128)}, f32[1024,256]{1,0:T(8,128)}, ...), condition=%wide.region_63.64_spmd, body=%wide.region_60.63_spmd.sunk | while | flops 19937348 | bytes 729607 | solution.py:108
  702.8 3.6 fusion.205
  720.4 29.0 %all-to-all-start.11 = ((f32[16,64,256]{2,1,0:T(8,128)}), f32[16,64,256]{2,1,0:T(8,128)}, u32[]{:S(2)}, u32[]{:S(2)}) async-start(f32[16,64,256]{2,1,0:T(8,128)} %bitcast.408), calls=%async_computation.11 | async-start | bytes 2097152 | tf_op jit(solution)/shard_map/all_to_all | solution.py:53
  755.1 11.5 %fusion.149 = f32[320,1,64]{2,1,0:T(1,128)S(1)} fusion(f32[320,64,1]{1,2,0:T(1,128)S(1)} %bitcast.414, f32[320,64,64]{2,1,0:T(8,128)} %copy.31), kind=kOutput, calls=%fused_computation.432 | convolution fusion | flops 15728640 | bytes 5406720 | tf_op jit(solution)/shard_map/ckl,ck->cl/dot_general | solution.py:159
  771.1 5.6 all-to-all-start.13
  777.9 3.8 all-to-all-done.13
  (557 shorter events, 242.3 us)
Async XLA Ops:
  7.2 10.6 %copy-start = (f32[8,64,1536]{2,1,0:T(8,128)S(1)}, f32[8,64,1536]{2,1,0:T(8,128)}, u32[]{:S(2)}) copy-start(f32[8,64,1536]{2,1,0:T(8,128)} %param.21) | copy-start | bytes 9437188
  7.2 53.7 %all-gather.2.cloned.1.call-start = ((), (), s32[]{:S(2)}) async-start(), calls=%async_computation.14 | async-start | bytes 3342336 | tf_op jit(solution)/shard_map/all_gather | solution.py:147
  9.4 14.8 %all-to-all-start = ((s32[16,1,1,72]{3,2,1,0:T(1,128)}), s32[16,1,1,72]{3,2,1,0:T(1,128)S(1)}, u32[]{:S(2)}, u32[]{:S(2)}) async-start(s32[16,1,1,72]{3,2,1,0:T(1,128)} %broadcast_in_dim.201), calls=%async_computation | async-start | bytes 16384 | tf_op jit(solution)/shard_map/all_to_all | solution.py:23
  24.2 88.8 %all-to-all-start.2 = ((f32[16,1,512]{2,1,0:T(1,128)}), f32[16,1,512]{2,1,0:T(1,128)S(1)}, u32[]{:S(2)}, u32[]{:S(2)}) async-start(f32[16,1,512]{2,1,0:T(1,128)} %reshape.846), calls=%async_computation.2 | async-start | bytes 65536 | tf_op jit(solution)/shard_map/all_to_all | solution.py:23
  59.1 8.8 %copy-start.1 = (f32[8,1536]{1,0:T(8,128)S(1)}, f32[8,1536]{1,0:T(8,128)}, u32[]{:S(2)}) copy-start(f32[8,1536]{1,0:T(8,128)} %param.18) | copy-start | bytes 147460
  113.0 40.1 %copy-start.3 = (s32[1152]{0:T(1024)}, s32[1152]{0:T(1024)S(1)}, u32[]{:S(2)}) copy-start(s32[1152]{0:T(1024)S(1)} %get-tuple-element.1530) | copy-start | bytes 13828
  113.0 27.6 %copy-start.16 = (s32[1,1,320]{2,1,0:T(1,128)S(1)}, s32[1,1,320]{2,1,0:T(1,128)}, u32[]{:S(2)}) copy-start(s32[1,1,320]{2,1,0:T(1,128)} %param.25) | copy-start | bytes 3844
  113.0 69.2 %all-to-all-start.1 = ((f32[16,64,256]{2,1,0:T(8,128)}), f32[16,64,256]{2,1,0:T(8,128)}, u32[]{:S(2)}, u32[]{:S(2)}) async-start(f32[16,64,256]{2,1,0:T(8,128)} %bitcast.406), calls=%async_computation.1 | async-start | bytes 2097152 | tf_op jit(solution)/shard_map/all_to_all | solution.py:53
  140.6 47.8 %copy-start.14 = (s32[320]{0:T(512)}, s32[320]{0:T(512)S(1)}, u32[]{:S(2)}) copy-start(s32[320]{0:T(512)S(1)} %get-tuple-element.699) | copy-start | bytes 3844
  140.7 83.5 %copy-start.15 = (s32[320]{0:T(512)}, s32[320]{0:T(512)S(1)}, u32[]{:S(2)}) copy-start(s32[320]{0:T(512)S(1)} %get-tuple-element.698) | copy-start | bytes 3844
  165.6 14.1 %copy-start.7 = (s32[1024]{0:T(1024)}, s32[1024]{0:T(1024)S(1)}, u32[]{:S(2)}) copy-start(s32[1024]{0:T(1024)S(1)} %pad_clamp_fusion.12) | copy-start | bytes 12292
  165.7 46.2 %copy-start.10 = (pred[320]{0:T(512)(128)(4,1)}, pred[320]{0:T(512)(128)(4,1)S(1)}, u32[]{:S(2)}) copy-start(pred[320]{0:T(512)(128)(4,1)S(1)} %compare_reduce_fusion) | copy-start | bytes 964
  184.1 9.3 %all-to-all-start.3 = ((f32[8,8,320]{2,1,0:T(8,128)}), f32[8,8,320]{2,1,0:T(8,128)S(1)}, u32[]{:S(2)}, u32[]{:S(2)}) async-start(f32[8,8,320]{2,1,0:T(8,128)} %maximum_bitcast_fusion), calls=%async_computation.3 | async-start | bytes 196608 | tf_op jit(solution)/shard_map/all_to_all | solution.py:53
  188.4 35.8 %copy-start.13 = (s32[1024]{0:T(1024)}, s32[1024]{0:T(1024)S(1)}, u32[]{:S(2)}) copy-start(s32[1024]{0:T(1024)S(1)} %pad_clamp_fusion.11) | copy-start | bytes 12292
  227.7 12.9 %all-to-all-start.5 = ((f32[16,1,512]{2,1,0:T(1,128)}), f32[16,1,512]{2,1,0:T(1,128)S(1)}, u32[]{:S(2)}, u32[]{:S(2)}) async-start(f32[16,1,512]{2,1,0:T(1,128)} %reshape.848), calls=%async_computation.5 | async-start | bytes 65536 | tf_op jit(solution)/shard_map/all_to_all | solution.py:53
  241.7 19.7 %all-to-all-start.4 = ((f32[16,64,256]{2,1,0:T(8,128)}), f32[16,64,256]{2,1,0:T(8,128)}, u32[]{:S(2)}, u32[]{:S(2)}) async-start(f32[16,64,256]{2,1,0:T(8,128)} %broadcast_in_dim.208), calls=%async_computation.4 | async-start | bytes 2097152 | tf_op jit(solution)/shard_map/all_to_all | solution.py:23
  246.0 15.4 %copy-start.4 = (s32[1152]{0:T(1024)S(1)}, s32[1152]{0:T(1024)}, u32[]{:S(2)}) copy-start(s32[1152]{0:T(1024)} %copy-done.3) | copy-start | bytes 13828
  361.1 50.8 %all-to-all-start.7 = ((f32[16,1,512]{2,1,0:T(1,128)}), f32[16,1,512]{2,1,0:T(1,128)S(1)}, u32[]{:S(2)}, u32[]{:S(2)}) async-start(f32[16,1,512]{2,1,0:T(1,128)} %reshape.850), calls=%async_computation.7 | async-start | bytes 65536 | tf_op jit(solution)/shard_map/all_to_all | solution.py:23
  411.9 42.7 %copy-start.5 = (s32[1152]{0:T(1024)}, s32[1152]{0:T(1024)S(1)}, u32[]{:S(2)}) copy-start(s32[1152]{0:T(1024)S(1)} %get-tuple-element.1532) | copy-start | bytes 13828
  411.9 30.0 %copy-start.8 = (s32[1024]{0:T(1024)S(1)}, s32[1024]{0:T(1024)}, u32[]{:S(2)}) copy-start(s32[1024]{0:T(1024)} %copy-done.7) | copy-start | bytes 12292
  411.9 31.1 %copy-start.11 = (pred[320]{0:T(512)(128)(4,1)S(1)}, pred[320]{0:T(512)(128)(4,1)}, u32[]{:S(2)}) copy-start(pred[320]{0:T(512)(128)(4,1)} %copy-done.10) | copy-start | bytes 964
  411.9 45.3 %all-to-all-start.6 = ((f32[16,64,256]{2,1,0:T(8,128)}), f32[16,64,256]{2,1,0:T(8,128)}, u32[]{:S(2)}, u32[]{:S(2)}) async-start(f32[16,64,256]{2,1,0:T(8,128)} %bitcast.407), calls=%async_computation.6 | async-start | bytes 2097152 | tf_op jit(solution)/shard_map/all_to_all | solution.py:53
  539.5 9.9 %all-to-all-start.10 = ((f32[16,1,512]{2,1,0:T(1,128)}), f32[16,1,512]{2,1,0:T(1,128)S(1)}, u32[]{:S(2)}, u32[]{:S(2)}) async-start(f32[16,1,512]{2,1,0:T(1,128)} %reshape.852), calls=%async_computation.10 | async-start | bytes 65536 | tf_op jit(solution)/shard_map/all_to_all | solution.py:53
  550.4 19.8 %all-to-all-start.9 = ((f32[16,64,256]{2,1,0:T(8,128)}), f32[16,64,256]{2,1,0:T(8,128)}, u32[]{:S(2)}, u32[]{:S(2)}) async-start(f32[16,64,256]{2,1,0:T(8,128)} %broadcast_in_dim.210), calls=%async_computation.9 | async-start | bytes 2097152 | tf_op jit(solution)/shard_map/all_to_all | solution.py:23
  554.8 15.5 %copy-start.6 = (s32[1152]{0:T(1024)S(1)}, s32[1152]{0:T(1024)}, u32[]{:S(2)}) copy-start(s32[1152]{0:T(1024)} %copy-done.5) | copy-start | bytes 13828
  670.1 50.3 %all-to-all-start.12 = ((f32[16,1,512]{2,1,0:T(1,128)}), f32[16,1,512]{2,1,0:T(1,128)S(1)}, u32[]{:S(2)}, u32[]{:S(2)}) async-start(f32[16,1,512]{2,1,0:T(1,128)} %reshape.854), calls=%async_computation.12 | async-start | bytes 65536 | tf_op jit(solution)/shard_map/all_to_all | solution.py:23
  720.4 46.2 %copy-start.2 = (f32[8,1536]{1,0:T(8,128)}, f32[8,1536]{1,0:T(8,128)S(1)}, u32[]{:S(2)}) copy-start(f32[8,1536]{1,0:T(8,128)S(1)} %get-tuple-element.1496) | copy-start | bytes 147460
  720.4 33.5 %copy-start.9 = (s32[1024]{0:T(1024)S(1)}, s32[1024]{0:T(1024)}, u32[]{:S(2)}) copy-start(s32[1024]{0:T(1024)} %copy-done.7) | copy-start | bytes 12292
  720.4 34.6 %copy-start.12 = (pred[320]{0:T(512)(128)(4,1)S(1)}, pred[320]{0:T(512)(128)(4,1)}, u32[]{:S(2)}) copy-start(pred[320]{0:T(512)(128)(4,1)} %copy-done.10) | copy-start | bytes 964
  720.4 48.8 %all-to-all-start.11 = ((f32[16,64,256]{2,1,0:T(8,128)}), f32[16,64,256]{2,1,0:T(8,128)}, u32[]{:S(2)}, u32[]{:S(2)}) async-start(f32[16,64,256]{2,1,0:T(8,128)} %bitcast.408), calls=%async_computation.11 | async-start | bytes 2097152 | tf_op jit(solution)/shard_map/all_to_all | solution.py:53
  771.1 10.6 %all-to-all-start.13 = ((f32[8,8,320]{2,1,0:T(8,128)}), f32[8,8,320]{2,1,0:T(8,128)S(1)}, u32[]{:S(2)}, u32[]{:S(2)}) async-start(f32[8,8,320]{2,1,0:T(8,128)} %maximum_bitcast_fusion.2), calls=%async_computation.13 | async-start | bytes 196608 | tf_op jit(solution)/shard_map/all_to_all | solution.py:53
Sparse Core Ops, SparseCore 0:
  10.2 50.6 all-gather.1
where the time goes:
time: 803 us; the launch traced here: 791 us
  blocking collectives  172 us (21%)
  local copies, waits for them, and re-layouts  165 us (21%)
  other arithmetic  163 us (20%)
  starting transfers between devices  136 us (17%)
  matrix products  78.4 us (10%)
  waiting for transfers between devices  51.3 us (6%)
  between operations  22.9 us (3%)
    psum x12, blocking collectives, over_axes(): value = lax.psum(value, axis)  131 us
    all_to_all x7, starting transfers between devices, summed_on_arrival(): lax.all_to_all(pieces, axis, split_axis=0, concat_axis=0, tiled=True)  106 us
    gather x40, local copies, waits for them, and re-layouts, one_group(): tensor = tensor_parts(obs_pts[obs_take], src_pts[src_take])  66.8 us
    reduce_sum x12, other arithmetic, one_group(): return running.at[src_take].add(jnp.sum(weighted, axis=1))  42.9 us
    dot_general x3, matrix products, far_adjoint(): jnp.einsum('ckl,ck->cl', coupling, chosen_coeffs, precision=exact)  34.6 us
    scatter-add x12, other arithmetic, one_group(): return running.at[src_take].add(jnp.sum(weighted, axis=1))  33.8 us
    reduce_sum x8, other arithmetic, one_group(): jnp.sum(component * strengths, axis=2)  33.7 us
    all_gather x2, blocking collectives, side_by_side(): lax.all_gather(both, axis, axis=dim, tiled=True)  31 us
  transfers between devices with their start and end apart: 14, of which 8 were waited for; matrix products, arithmetic and copies ran while one was open for 33% of the time, Pallas kernels for 0%

commit v1 on v0

--- a/solution.py
+++ b/solution.py
@@ -12,9 +12,15 @@
 exact = lax.Precision.HIGHEST
 
 
+def summed_here(x, axis):
+    parts = lax.all_gather(x, axis, axis=0, tiled=False)
+    result = parts.sum(axis=0)
+    return result
+
+
 def over_axes(value, axes):
     for axis in axes:
-        value = lax.psum(value, axis)
+        value = summed_here(value, axis)
     return value
 
 

time: 803 us -> 848 us (1.056)
  local copies, waits for them, and re-layouts: 165 us -> 206 us
  other arithmetic: 163 us -> 179 us
  blocking collectives: 172 us -> 163 us
    psum x12 -> x0, blocking collectives: 131 us -> none  [over_axes(): value = lax.psum(value, axis)]
    unnamed x0 -> x12, blocking collectives: none -> 123 us
    unnamed x45 -> x113, local copies, waits for them, and re-layouts: 4.07 us -> 45.6 us
    reduce_sum x0 -> x28, other arithmetic: none -> 16.9 us  [summed_here(): result = parts.sum(axis=0)]
  transfers between devices with their start and end apart: 14 -> 14, of which waited for: 8 -> 8; matrix products, arithmetic and copies ran while one was open for 33% -> 32% of each run, Pallas kernels for 0% -> 0%
where the time goes in v1:
time: 848 us; the launch traced here: 836 us
  local copies, waits for them, and re-layouts  206 us (24%)
  other arithmetic  179 us (21%)
  blocking collectives  163 us (19%)
  starting transfers between devices  137 us (16%)
  matrix products  78.4 us (9%)
  waiting for transfers between devices  46.8 us (6%)
  between operations  22.7 us (3%)
    unnamed x12, blocking collectives  123 us
    all_to_all x7, starting transfers between devices, summed_on_arrival(): lax.all_to_all(pieces, axis, split_axis=0, concat_axis=0, tiled=True)  106 us
    gather x40, local copies, waits for them, and re-layouts, one_group(): tensor = tensor_parts(obs_pts[obs_take], src_pts[src_take])  66.8 us
    unnamed x113, local copies, waits for them, and re-layouts  45.6 us
    reduce_sum x12, other arithmetic, one_group(): return running.at[src_take].add(jnp.sum(weighted, axis=1))  42.9 us
    dot_general x3, matrix products, far_adjoint(): jnp.einsum('ckl,ck->cl', coupling, chosen_coeffs, precision=exact)  34.6 us
    reduce_sum x8, other arithmetic, one_group(): jnp.sum(component * strengths, axis=2)  33.7 us
    scatter-add x12, other arithmetic, one_group(): return running.at[src_take].add(jnp.sum(weighted, axis=1))  33.4 us
  transfers between devices with their start and end apart: 14, of which 8 were waited for; matrix products, arithmetic and copies ran while one was open for 32% of the time, Pallas kernels for 0%

profile of v1, /device:TPU:1, one launch (start us, length us, event | category | flops | bytes accessed | tf_op | source)
XLA Modules:
  0.0 835.9 jit_solution(41711639222879449)
XLA Ops:
  9.4 8.4 %all-to-all-start = ((s32[16,1,1,72]{3,2,1,0:T(1,128)}), s32[16,1,1,72]{3,2,1,0:T(1,128)S(1)}, u32[]{:S(2)}, u32[]{:S(2)}) async-start(s32[16,1,1,72]{3,2,1,0:T(1,128)} %broadcast_in_dim.201), calls=%async_computation | async-start | bytes 16384 | tf_op jit(solution)/shard_map/all_to_all | solution.py:29
  24.2 5.4 all-to-all-start.2
  33.1 6.4 scatter_custom_fusion.5
  39.6 6.5 gather_fusion.16
  46.1 6.5 gather_fusion.17
  52.6 6.5 gather_fusion.15
  60.9 6.0 copy.23
  67.9 45.0 %while.60 = (s32[]{:T(128)}, f32[1024,256]{1,0:T(8,128)}, s32[]{:T(128)}, s32[1152]{0:T(1024)S(1)}, s32[1152]{0:T(1024)S(1)}, /*index=5*/f32[8,3,256]{2,1,0:T(4,...) while((s32[]{:T(128)}, f32[1024,256]{1,0:T(8,128)}, ...), condition=%wide.region_7.8_spmd, body=%wide.region_4.7_spmd.sunk | while | flops 19937348 | bytes 729607 | solution.py:114
  113.0 27.9 %all-to-all-start.1 = ((f32[16,64,256]{2,1,0:T(8,128)}), f32[16,64,256]{2,1,0:T(8,128)}, u32[]{:S(2)}, u32[]{:S(2)}) async-start(f32[16,64,256]{2,1,0:T(8,128)} %bitcast.438), calls=%async_computation.1 | async-start | bytes 2097152 | tf_op jit(solution)/shard_map/all_to_all | solution.py:59
  140.9 12.4 %copy.31 = f32[320,64,64]{2,1,0:T(8,128)} copy(f32[320,64,64]{0,2,1:T(8,128)} %bitcast.436) | data formatting | bytes 10485760 | tf_op jit(solution)/shard_map/squeeze | solution.py:146
  153.3 12.5 %copy.38 = f32[320,64,64]{1,2,0:T(8,128)} copy(f32[320,64,64]{0,2,1:T(8,128)} %bitcast.437) | data formatting | bytes 10485760 | tf_op jit(solution)/shard_map/squeeze | solution.py:146
  168.4 11.5 %fusion.141 = f32[320,1,64]{2,1,0:T(1,128)S(1)} fusion(f32[320,64,1]{1,2,0:T(1,128)S(1)} %bitcast.448, f32[320,64,64]{2,1,0:T(8,128)} %copy.31), kind=kOutput, calls=%fused_computation.424 | convolution fusion | flops 15728640 | bytes 5406720 | tf_op jit(solution)/shard_map/ckl,ck->cl/dot_general | solution.py:165
  184.4 4.3 all-to-all-start.3
  188.7 5.0 all-to-all-done.3
  197.3 13.6 %all_gather.186 = f32[64,320]{1,0:T(8,128)S(1)} all-gather(f32[8,320]{1,0:T(8,128)S(1)} %pad_maximum_fusion), channel_id=1, replica_groups=mesh['obs_0'=4,'obs_1'=2,'src_0'=4,'src_1'=4] {'obs_0','obs_1'}, dimensions={0}, use_global_device_ids=true | all-gather | bytes 92160 | tf_op jit(solution)/shard_map/all_gather | solution.py:49
  212.0 12.2 %fusion.143 = f32[320,1,64]{2,1,0:T(1,128)} fusion(f32[320,64,1]{1,2,0:T(1,128)S(1)} %bitcast.449, f32[320,64,64]{1,2,0:T(8,128)} %copy.38), kind=kOutput, calls=%fused_computation.426 | convolution fusion | flops 15728640 | bytes 5406720 | tf_op jit(solution)/shard_map/ckl,cl->ck/dot_general | solution.py:198
  227.7 6.4 all-to-all-start.5
  234.2 6.5 all-to-all-done.5
  241.7 4.4 all-to-all-start.4
  250.4 11.0 %all-to-all-done.4 = f32[16,64,256]{2,1,0:T(8,128)} async-done(((f32[16,64,256]{2,1,0:T(8,128)}), f32[16,64,256]{2,1,0:T(8,128)}, u32[]{:S(2)}, u32[]{:S(2)}) %all-to-all-start.4) | async-done | bytes 1048608 | tf_op jit(solution)/shard_map/all_to_all | solution.py:29
  261.5 44.4 %while.61 = (s32[]{:T(128)}, f32[8,1536]{1,0:T(8,128)S(1)}, s32[]{:T(128)}, s32[1152]{0:T(1024)S(1)}, f32[8,3,256]{2,1,0:T(4,128)S(1)}, /*index=5*/s32[1152]{0:T...) while((s32[]{:T(128)}, f32[8,1536]{1,0:T(8,128)S(1)}, ...), condition=%wide.region_24.25_spmd, body=%wide.region_16.24_spmd.sunk | while | flops 19927108 | bytes 688647 | solution.py:114
  267.6 4.2 fusion.196
  278.7 4.2 fusion.196
  289.9 4.2 fusion.196
  301.0 4.2 fusion.196
  308.6 18.3 %all-reduce.33 = (f32[4]{0:T(128)S(1)}, f32[4]{0:T(128)S(1)}) all-reduce(f32[4]{0:T(128)S(1)} %dynamic-update-slice, f32[4]{0:T(128)S(1)} %dynamic-update-slice.4), channel_id=1, replica_groups=mesh['obs_0'=4,'obs_1'=2,'src_0'=4,'src_1'=4] {'obs_0'}, use_global_device_ids=true, to_apply=%add | all-reduce | flops 8 | bytes 64
  331.4 16.7 %all-reduce.35 = (f32[2]{0:T(128)S(1)}, f32[2]{0:T(128)S(1)}) all-reduce(f32[2]{0:T(128)S(1)} %dynamic-update-slice.1, f32[2]{0:T(128)S(1)} %dynamic-update-slice.5), channel_id=1, replica_groups=mesh['obs_0'=4,'obs_1'=2,'src_0'=4,'src_1'=4] {'obs_1'}, use_global_device_ids=true, to_apply=%add.1 | all-reduce | flops 4 | bytes 32
  353.2 6.1 all-reduce.31
  363.2 6.0 all-reduce.29
  374.9 4.2 all-to-all-start.7
  380.2 45.0 %while.62 = (s32[]{:T(128)}, f32[1024,256]{1,0:T(8,128)}, s32[]{:T(128)}, s32[1152]{0:T(1024)S(1)}, s32[1152]{0:T(1024)S(1)}, /*index=5*/f32[8,3,256]{2,1,0:T(4,...) while((s32[]{:T(128)}, f32[1024,256]{1,0:T(8,128)}, ...), condition=%wide.region_35.36_spmd, body=%wide.region_32.35_spmd.sunk | while | flops 19937348 | bytes 729607 | solution.py:114
  385.1 3.6 fusion.199
  396.4 3.6 fusion.199
  425.3 29.0 %all-to-all-start.6 = ((f32[16,64,256]{2,1,0:T(8,128)}), f32[16,64,256]{2,1,0:T(8,128)}, u32[]{:S(2)}, u32[]{:S(2)}) async-start(f32[16,64,256]{2,1,0:T(8,128)} %bitcast.439), calls=%async_computation.6 | async-start | bytes 2097152 | tf_op jit(solution)/shard_map/all_to_all | solution.py:59
  456.2 11.5 %fusion.145 = f32[320,1,64]{2,1,0:T(1,128)S(1)} fusion(f32[320,64,1]{1,2,0:T(1,128)S(1)} %bitcast.450, f32[320,64,64]{2,1,0:T(8,128)} %copy.31), kind=kOutput, calls=%fused_computation.428 | convolution fusion | flops 15728640 | bytes 5406720 | tf_op jit(solution)/shard_map/ckl,ck->cl/dot_general | solution.py:165
  471.7 9.7 %all_to_all.70 = f32[8,8,320]{2,1,0:T(8,128)S(1)} all-to-all(f32[8,8,320]{2,1,0:T(8,128)S(1)} %maximum_bitcast_fusion.1), channel_id=1, replica_groups=mesh['obs_0'=4,'obs_1'=2,'src_0'=4,'src_1'=4] {'obs_0','obs_1'}, dimensions={0} | all-to-all | bytes 163840 | tf_op jit(solution)/shard_map/all_to_all | solution.py:59
  484.8 6.8 all-reduce.8
  493.6 4.9 all-reduce.9
  500.6 8.7 %all-reduce.10 = f32[4]{0:T(128)S(1)} all-reduce(f32[4]{0:T(128)S(1)} %dynamic-update-slice.10), channel_id=1, replica_groups=mesh['obs_0'=4,'obs_1'=2,'src_0'=4,'src_1'=4] {'src_0'}, use_global_device_ids=true, to_apply=%add.10 | all-reduce | flops 4 | bytes 32
  511.2 8.6 %all-reduce.11 = f32[4]{0:T(128)S(1)} all-reduce(f32[4]{0:T(128)S(1)} %dynamic-update-slice.11), channel_id=1, replica_groups=mesh['obs_0'=4,'obs_1'=2,'src_0'=4,'src_1'=4] {'src_1'}, use_global_device_ids=true, to_apply=%add.11 | all-reduce | flops 4 | bytes 32
  523.3 17.0 %all_gather.203 = f32[64,320]{1,0:T(8,128)S(1)} all-gather(f32[8,320]{1,0:T(8,128)S(1)} %pad_maximum_fusion.1), channel_id=1, replica_groups=mesh['obs_0'=4,'obs_1'=2,'src_0'=4,'src_1'=4] {'obs_0','obs_1'}, dimensions={0}, use_global_device_ids=true | all-gather | bytes 92160 | tf_op jit(solution)/shard_map/all_gather | solution.py:49
  542.2 12.2 %fusion.147 = f32[320,1,64]{2,1,0:T(1,128)} fusion(f32[320,64,1]{1,2,0:T(1,128)S(1)} %bitcast.447, f32[320,64,64]{1,2,0:T(8,128)} %copy.38), kind=kOutput, calls=%fused_computation.430 | convolution fusion | flops 15728640 | bytes 5406720 | tf_op jit(solution)/shard_map/ckl,cl->ck/dot_general | solution.py:198
  561.4 6.4 all-to-all-done.10
  568.8 4.3 all-to-all-start.9
  578.3 10.4 %all-to-all-done.9 = f32[16,64,256]{2,1,0:T(8,128)} async-done(((f32[16,64,256]{2,1,0:T(8,128)}), f32[16,64,256]{2,1,0:T(8,128)}, u32[]{:S(2)}, u32[]{:S(2)}) %all-to-all-start.9) | async-done | bytes 1048608 | tf_op jit(solution)/shard_map/all_to_all | solution.py:29
  588.7 44.4 %while.63 = (s32[]{:T(128)}, f32[8,1536]{1,0:T(8,128)S(1)}, s32[]{:T(128)}, s32[1152]{0:T(1024)S(1)}, f32[8,3,256]{2,1,0:T(4,128)S(1)}, /*index=5*/s32[1152]{0:T...) while((s32[]{:T(128)}, f32[8,1536]{1,0:T(8,128)S(1)}, ...), condition=%wide.region_52.53_spmd, body=%wide.region_44.52_spmd.sunk | while | flops 19927108 | bytes 688647 | solution.py:114
  594.8 4.2 fusion.202
  605.9 4.2 fusion.202
  617.0 4.2 fusion.202
  628.1 4.2 fusion.202
  636.7 17.9 %all-reduce.32 = (f32[4]{0:T(128)S(1)}, f32[4]{0:T(128)S(1)}, f32[4]{0:T(128)S(1)}, f32[4]{0:T(128)S(1)}) all-reduce(f32[4]{0:T(128)S(1)} %dynamic-update-slice.12, f32[4]{0:T(128)S(1)} %dynamic-update-slice.16, f32[4]{0:T(128)S(1)} %dynamic-update-slice.20, ...), channel_id=1, replica_groups=mesh['obs_0'=4,'obs_1'=2,'src_0'=4,'src_1'=4] {'obs_0'}, use_global_device_ids=true, to_apply=%add.12 | all-reduce | flops 16 | bytes 128
  662.4 17.1 %all-reduce.34 = (f32[2]{0:T(128)S(1)}, f32[2]{0:T(128)S(1)}, f32[2]{0:T(128)S(1)}, f32[2]{0:T(128)S(1)}) all-reduce(f32[2]{0:T(128)S(1)} %dynamic-update-slice.13, f32[2]{0:T(128)S(1)} %dynamic-update-slice.17, f32[2]{0:T(128)S(1)} %dynamic-update-slice.21, ...), channel_id=1, replica_groups=mesh['obs_0'=4,'obs_1'=2,'src_0'=4,'src_1'=4] {'obs_1'}, use_global_device_ids=true, to_apply=%add.13 | all-reduce | flops 8 | bytes 64
  687.7 6.1 all-reduce.30
  701.6 6.0 all-reduce.28
  713.0 4.2 all-to-all-start.12
  718.2 45.0 %while.64 = (s32[]{:T(128)}, f32[1024,256]{1,0:T(8,128)}, s32[]{:T(128)}, s32[1152]{0:T(1024)S(1)}, s32[1152]{0:T(1024)S(1)}, /*index=5*/f32[8,3,256]{2,1,0:T(4,...) while((s32[]{:T(128)}, f32[1024,256]{1,0:T(8,128)}, ...), condition=%wide.region_63.64_spmd, body=%wide.region_60.63_spmd.sunk | while | flops 19937348 | bytes 729607 | solution.py:114
  723.1 3.6 fusion.205
  734.4 3.6 fusion.205
  745.6 3.6 fusion.205
  756.9 3.6 fusion.205
  763.3 29.2 %all-to-all-start.11 = ((f32[16,64,256]{2,1,0:T(8,128)}), f32[16,64,256]{2,1,0:T(8,128)}, u32[]{:S(2)}, u32[]{:S(2)}) async-start(f32[16,64,256]{2,1,0:T(8,128)} %bitcast.440), calls=%async_computation.11 | async-start | bytes 2097152 | tf_op jit(solution)/shard_map/all_to_all | solution.py:59
  800.1 11.5 %fusion.149 = f32[320,1,64]{2,1,0:T(1,128)S(1)} fusion(f32[320,64,1]{1,2,0:T(1,128)S(1)} %bitcast.446, f32[320,64,64]{2,1,0:T(8,128)} %copy.31), kind=kOutput, calls=%fused_computation.432 | convolution fusion | flops 15728640 | bytes 5406720 | tf_op jit(solution)/shard_map/ckl,ck->cl/dot_general | solution.py:165
  816.2 5.6 all-to-all-start.13
  823.0 3.8 all-to-all-done.13
  (653 shorter events, 300.2 us)
Async XLA Ops:
  7.2 10.6 %copy-start = (f32[8,64,1536]{2,1,0:T(8,128)S(1)}, f32[8,64,1536]{2,1,0:T(8,128)}, u32[]{:S(2)}) copy-start(f32[8,64,1536]{2,1,0:T(8,128)} %param.21) | copy-start | bytes 9437188
  7.2 53.7 %all-gather.2.cloned.1.call-start = ((), (), s32[]{:S(2)}) async-start(), calls=%async_computation.14 | async-start | bytes 3342336 | tf_op jit(solution)/shard_map/all_gather | solution.py:153
  9.4 14.8 %all-to-all-start = ((s32[16,1,1,72]{3,2,1,0:T(1,128)}), s32[16,1,1,72]{3,2,1,0:T(1,128)S(1)}, u32[]{:S(2)}, u32[]{:S(2)}) async-start(s32[16,1,1,72]{3,2,1,0:T(1,128)} %broadcast_in_dim.201), calls=%async_computation | async-start | bytes 16384 | tf_op jit(solution)/shard_map/all_to_all | solution.py:29
  24.2 88.8 %all-to-all-start.2 = ((f32[16,1,512]{2,1,0:T(1,128)}), f32[16,1,512]{2,1,0:T(1,128)S(1)}, u32[]{:S(2)}, u32[]{:S(2)}) async-start(f32[16,1,512]{2,1,0:T(1,128)} %reshape.986), calls=%async_computation.2 | async-start | bytes 65536 | tf_op jit(solution)/shard_map/all_to_all | solution.py:29
  59.1 8.8 %copy-start.1 = (f32[8,1536]{1,0:T(8,128)S(1)}, f32[8,1536]{1,0:T(8,128)}, u32[]{:S(2)}) copy-start(f32[8,1536]{1,0:T(8,128)} %param.18) | copy-start | bytes 147460
  113.0 40.4 %copy-start.3 = (s32[1152]{0:T(1024)}, s32[1152]{0:T(1024)S(1)}, u32[]{:S(2)}) copy-start(s32[1152]{0:T(1024)S(1)} %get-tuple-element.1530) | copy-start | bytes 13828
  113.0 27.9 %copy-start.16 = (s32[1,1,320]{2,1,0:T(1,128)S(1)}, s32[1,1,320]{2,1,0:T(1,128)}, u32[]{:S(2)}) copy-start(s32[1,1,320]{2,1,0:T(1,128)} %param.25) | copy-start | bytes 3844
  113.0 69.4 %all-to-all-start.1 = ((f32[16,64,256]{2,1,0:T(8,128)}), f32[16,64,256]{2,1,0:T(8,128)}, u32[]{:S(2)}, u32[]{:S(2)}) async-start(f32[16,64,256]{2,1,0:T(8,128)} %bitcast.438), calls=%async_computation.1 | async-start | bytes 2097152 | tf_op jit(solution)/shard_map/all_to_all | solution.py:59
  140.9 47.8 %copy-start.14 = (s32[320]{0:T(512)}, s32[320]{0:T(512)S(1)}, u32[]{:S(2)}) copy-start(s32[320]{0:T(512)S(1)} %get-tuple-element.699) | copy-start | bytes 3844
  140.9 83.3 %copy-start.15 = (s32[320]{0:T(512)}, s32[320]{0:T(512)S(1)}, u32[]{:S(2)}) copy-start(s32[320]{0:T(512)S(1)} %get-tuple-element.698) | copy-start | bytes 3844
  165.9 14.1 %copy-start.7 = (s32[1024]{0:T(1024)}, s32[1024]{0:T(1024)S(1)}, u32[]{:S(2)}) copy-start(s32[1024]{0:T(1024)S(1)} %pad_clamp_fusion.12) | copy-start | bytes 12292
  165.9 46.0 %copy-start.10 = (pred[320]{0:T(512)(128)(4,1)}, pred[320]{0:T(512)(128)(4,1)S(1)}, u32[]{:S(2)}) copy-start(pred[320]{0:T(512)(128)(4,1)S(1)} %compare_reduce_fusion) | copy-start | bytes 964
  184.4 9.3 %all-to-all-start.3 = ((f32[8,8,320]{2,1,0:T(8,128)}), f32[8,8,320]{2,1,0:T(8,128)S(1)}, u32[]{:S(2)}, u32[]{:S(2)}) async-start(f32[8,8,320]{2,1,0:T(8,128)} %maximum_bitcast_fusion), calls=%async_computation.3 | async-start | bytes 196608 | tf_op jit(solution)/shard_map/all_to_all | solution.py:59
  188.7 35.6 %copy-start.13 = (s32[1024]{0:T(1024)}, s32[1024]{0:T(1024)S(1)}, u32[]{:S(2)}) copy-start(s32[1024]{0:T(1024)S(1)} %pad_clamp_fusion.11) | copy-start | bytes 12292
  224.2 21.9 %copy-start.20 = (u32[128]{0:T(128)S(1)}, u32[128]{0:T(128)}, u32[]{:S(2)}) copy-start(u32[128]{0:T(128)} %constant.350) | copy-start | bytes 1540
  227.7 12.9 %all-to-all-start.5 = ((f32[16,1,512]{2,1,0:T(1,128)}), f32[16,1,512]{2,1,0:T(1,128)S(1)}, u32[]{:S(2)}, u32[]{:S(2)}) async-start(f32[16,1,512]{2,1,0:T(1,128)} %reshape.988), calls=%async_computation.5 | async-start | bytes 65536 | tf_op jit(solution)/shard_map/all_to_all | solution.py:59
  241.7 19.7 %all-to-all-start.4 = ((f32[16,64,256]{2,1,0:T(8,128)}), f32[16,64,256]{2,1,0:T(8,128)}, u32[]{:S(2)}, u32[]{:S(2)}) async-start(f32[16,64,256]{2,1,0:T(8,128)} %broadcast_in_dim.208), calls=%async_computation.4 | async-start | bytes 2097152 | tf_op jit(solution)/shard_map/all_to_all | solution.py:29
  246.1 15.4 %copy-start.4 = (s32[1152]{0:T(1024)S(1)}, s32[1152]{0:T(1024)}, u32[]{:S(2)}) copy-start(s32[1152]{0:T(1024)} %copy-done.3) | copy-start | bytes 13828
  261.5 46.5 %copy-start.19 = (u32[128]{0:T(128)S(1)}, u32[128]{0:T(128)}, u32[]{:S(2)}) copy-start(u32[128]{0:T(128)} %constant.355) | copy-start | bytes 1540
  261.5 69.2 %copy-start.18 = (u32[128]{0:T(128)S(1)}, u32[128]{0:T(128)}, u32[]{:S(2)}) copy-start(u32[128]{0:T(128)} %constant.360) | copy-start | bytes 1540
  261.5 91.1 %copy-start.17 = (u32[128]{0:T(128)S(1)}, u32[128]{0:T(128)}, u32[]{:S(2)}) copy-start(u32[128]{0:T(128)} %constant.365) | copy-start | bytes 1540
  374.9 50.3 %all-to-all-start.7 = ((f32[16,1,512]{2,1,0:T(1,128)}), f32[16,1,512]{2,1,0:T(1,128)S(1)}, u32[]{:S(2)}, u32[]{:S(2)}) async-start(f32[16,1,512]{2,1,0:T(1,128)} %reshape.990), calls=%async_computation.7 | async-start | bytes 65536 | tf_op jit(solution)/shard_map/all_to_all | solution.py:29
  425.2 42.5 %copy-start.5 = (s32[1152]{0:T(1024)}, s32[1152]{0:T(1024)S(1)}, u32[]{:S(2)}) copy-start(s32[1152]{0:T(1024)S(1)} %get-tuple-element.1532) | copy-start | bytes 13828
  425.2 29.8 %copy-start.8 = (s32[1024]{0:T(1024)S(1)}, s32[1024]{0:T(1024)}, u32[]{:S(2)}) copy-start(s32[1024]{0:T(1024)} %copy-done.7) | copy-start | bytes 12292
  425.2 30.9 %copy-start.11 = (pred[320]{0:T(512)(128)(4,1)S(1)}, pred[320]{0:T(512)(128)(4,1)}, u32[]{:S(2)}) copy-start(pred[320]{0:T(512)(128)(4,1)} %copy-done.10) | copy-start | bytes 964
  425.3 45.1 %all-to-all-start.6 = ((f32[16,64,256]{2,1,0:T(8,128)}), f32[16,64,256]{2,1,0:T(8,128)}, u32[]{:S(2)}, u32[]{:S(2)}) async-start(f32[16,64,256]{2,1,0:T(8,128)} %bitcast.439), calls=%async_computation.6 | async-start | bytes 2097152 | tf_op jit(solution)/shard_map/all_to_all | solution.py:59
  557.9 9.9 %all-to-all-start.10 = ((f32[16,1,512]{2,1,0:T(1,128)}), f32[16,1,512]{2,1,0:T(1,128)S(1)}, u32[]{:S(2)}, u32[]{:S(2)}) async-start(f32[16,1,512]{2,1,0:T(1,128)} %reshape.992), calls=%async_computation.10 | async-start | bytes 65536 | tf_op jit(solution)/shard_map/all_to_all | solution.py:59
  568.8 19.8 %all-to-all-start.9 = ((f32[16,64,256]{2,1,0:T(8,128)}), f32[16,64,256]{2,1,0:T(8,128)}, u32[]{:S(2)}, u32[]{:S(2)}) async-start(f32[16,64,256]{2,1,0:T(8,128)} %broadcast_in_dim.210), calls=%async_computation.9 | async-start | bytes 2097152 | tf_op jit(solution)/shard_map/all_to_all | solution.py:29
  573.2 15.5 %copy-start.6 = (s32[1152]{0:T(1024)S(1)}, s32[1152]{0:T(1024)}, u32[]{:S(2)}) copy-start(s32[1152]{0:T(1024)} %copy-done.5) | copy-start | bytes 13828
  713.0 50.3 %all-to-all-start.12 = ((f32[16,1,512]{2,1,0:T(1,128)}), f32[16,1,512]{2,1,0:T(1,128)S(1)}, u32[]{:S(2)}, u32[]{:S(2)}) async-start(f32[16,1,512]{2,1,0:T(1,128)} %reshape.994), calls=%async_computation.12 | async-start | bytes 65536 | tf_op jit(solution)/shard_map/all_to_all | solution.py:29
  763.3 48.4 %copy-start.2 = (f32[8,1536]{1,0:T(8,128)}, f32[8,1536]{1,0:T(8,128)S(1)}, u32[]{:S(2)}) copy-start(f32[8,1536]{1,0:T(8,128)S(1)} %get-tuple-element.1496) | copy-start | bytes 147460
  763.3 35.6 %copy-start.9 = (s32[1024]{0:T(1024)S(1)}, s32[1024]{0:T(1024)}, u32[]{:S(2)}) copy-start(s32[1024]{0:T(1024)} %copy-done.7) | copy-start | bytes 12292
  763.3 36.7 %copy-start.12 = (pred[320]{0:T(512)(128)(4,1)S(1)}, pred[320]{0:T(512)(128)(4,1)}, u32[]{:S(2)}) copy-start(pred[320]{0:T(512)(128)(4,1)} %copy-done.10) | copy-start | bytes 964
  763.3 51.0 %all-to-all-start.11 = ((f32[16,64,256]{2,1,0:T(8,128)}), f32[16,64,256]{2,1,0:T(8,128)}, u32[]{:S(2)}, u32[]{:S(2)}) async-start(f32[16,64,256]{2,1,0:T(8,128)} %bitcast.440), calls=%async_computation.11 | async-start | bytes 2097152 | tf_op jit(solution)/shard_map/all_to_all | solution.py:59
  816.2 10.6 %all-to-all-start.13 = ((f32[8,8,320]{2,1,0:T(8,128)}), f32[8,8,320]{2,1,0:T(8,128)S(1)}, u32[]{:S(2)}, u32[]{:S(2)}) async-start(f32[8,8,320]{2,1,0:T(8,128)} %maximum_bitcast_fusion.2), calls=%async_computation.13 | async-start | bytes 196608 | tf_op jit(solution)/shard_map/all_to_all | solution.py:59
Sparse Core Ops, SparseCore 0:
  10.2 50.6 all-gather.1
